TPU v7x, 32 devices: a whole 2x2x4 slice. The times are simulated.
32 devices in a mesh: lat: 8 (over z, x), lon: 4 (over y, core).
Axes of the slice: x: 2, y: 2, z: 4, core: 2. Of those that a mesh axis runs over, the one named last changes fastest.
Arguments:
- fields: float32 [8, 8, 128, 512], P(None, None, 'lat', 'lon'), may hold values from -6 to 6
- ocean_mask: int32 [128, 4], replicated, may hold values from 0 to 1, as said below
- scale_table: float32 [16], replicated, may hold values from 0.5 to 4
- offset_table: float32 [16], replicated, may hold values from -4 to 4
- scale_index: int32 [8], replicated, may hold values from 0 to 15
- offset_index: int32 [8], replicated, may hold values from 0 to 15
Outputs:
- history: float32 [8, 8, 128, 512], P(None, 'lat', 'lon')
- record_range: float32 [2, 8, 8], P(None, None, 'lat')
Inputs may be any that keep to these rules, and one draw needn't show every extreme that they name: `ocean_mask`: each device's block of 16 rows and 128 longitudes holds at least half of 12 (rounded down, and never fewer than one) and at most 12 ocean strips; some block holds exactly 12.
All inputs are finite; a program needn't handle non-finite values.
Results may differ from a plain program's by a relative error of at most 0.00007.
Values sent between devices are 32-bit elements; how exact they have to be, the bound alone decides.
A program may use at most 64 MiB of HBM per device.

v0:
```python
import functools

import jax
import jax.numpy as jnp
from jax import lax
from jax.experimental import pallas as pl
from jax.experimental.pallas import tpu as pltpu
from jax.sharding import PartitionSpec as P

STRIP = 128
MAX_LIVE = 12
MESH = pl.DeviceIdType.MESH


def kernel(
    dims, mask_hbm, scale_table_hbm, offset_table_hbm, scale_index_hbm, offset_index_hbm, x_hbm,
    out, rng,
    mask, scale_table, offset_table, scale_index, offset_index,
    xv, send, recv, stage, part, first_stats, last_stats,
    in_sem, send_sem, recv_sem, stat_send, stat_recv, last_send, last_recv, from_below, from_above,
):
    fields, levels, rows, lat_count, lon_count = dims
    slab = lat_count // lon_count
    planes = lat_count // slab
    plane_size = slab * lon_count
    slots = send.shape[1]
    lat_pos = lax.axis_index("lat")
    lon_pos = lax.axis_index("lon")
    plane = lat_pos // slab
    here = lax.rem(lat_pos, slab) * lon_count + lon_pos

    barrier = pltpu.get_barrier_semaphore()

    def greet(step, carry):
        other = lax.rem(here + step, plane_size)
        target = (plane * slab + other // lon_count, lax.rem(other, lon_count))
        pl.semaphore_signal(barrier, inc=1, device_id=target, device_id_type=MESH)
        return carry

    lax.fori_loop(1, plane_size, greet, 0)
    has_above = plane < planes - 1
    has_below = plane > 0

    def call_above(sem):
        @pl.when(has_above)
        def _():
            pl.semaphore_signal(sem, inc=1, device_id=(lat_pos + slab, lon_pos), device_id_type=MESH)

    def call_below(sem):
        @pl.when(has_below)
        def _():
            pl.semaphore_signal(sem, inc=1, device_id=(lat_pos - slab, lon_pos), device_id_type=MESH)

    call_above(barrier)
    call_below(barrier)

    load = pltpu.make_async_copy(x_hbm, xv, in_sem.at[0])
    smalls = [
        pltpu.make_async_copy(src, dst, in_sem.at[n + 1])
        for n, (src, dst) in enumerate([
            (mask_hbm, mask), (scale_table_hbm, scale_table), (offset_table_hbm, offset_table),
            (scale_index_hbm, scale_index), (offset_index_hbm, offset_index),
        ])
    ]
    for copy in smalls:
        copy.start()
    load.start()
    for copy in smalls:
        copy.wait()

    seen = []
    total = jnp.int32(0)
    for r in range(rows):
        total = total + mask[lon_pos, lat_pos * rows + r]
        seen.append(total)
    picks = []
    for k in range(slots):
        slot = jnp.minimum(k, total - 1)
        pick = jnp.int32(0)
        for r in range(rows - 1):
            pick = pick + (seen[r] <= slot).astype(jnp.int32)
        picks.append(pick)

    which = lax.broadcasted_iota(jnp.int32, (fields, STRIP), 0)
    scales = jnp.zeros((fields, STRIP), jnp.float32)
    offsets = jnp.zeros((fields, STRIP), jnp.float32)
    for f in range(fields):
        scales = jnp.where(which == f, scale_table[scale_index[f]], scales)
        offsets = jnp.where(which == f, offset_table[offset_index[f]], offsets)

    load.wait()

    def pack(level, carry):
        high = None
        for k in range(slots):
            strip = xv[pl.ds(level * rows + picks[k], fields, stride=levels * rows), :]
            packed = (strip - offsets) * scales
            send[level, k] = packed
            high = packed if k == 0 else jnp.maximum(high, packed)
            low = -packed if k == 0 else jnp.maximum(low, -packed)
        part[pl.ds(pl.multiple_of(level * fields, fields), fields), :] = high
        part[pl.ds(pl.multiple_of((levels + level) * fields, fields), fields), :] = low
        return carry

    lax.fori_loop(0, levels, pack, 0)

    neighbours = has_above.astype(jnp.int32) + has_below.astype(jnp.int32)
    pl.semaphore_wait(barrier, plane_size - 1 + neighbours)
    call_above(from_below)
    call_below(from_above)

    for j in range(first_stats.shape[1]):
        tile = part[j * STRIP:(j + 1) * STRIP, :].T
        first_stats[plane, j] = jnp.max(tile, axis=0, keepdims=True)

    def remote(level):
        return pltpu.make_async_remote_copy(
            src_ref=send.at[level],
            dst_ref=recv.at[here],
            send_sem=send_sem.at[level],
            recv_sem=recv_sem.at[here],
            device_id=(level, plane),
            device_id_type=MESH,
        )

    def tell(target):
        return pltpu.make_async_remote_copy(
            src_ref=first_stats.at[plane],
            dst_ref=first_stats.at[plane],
            send_sem=stat_send.at[target],
            recv_sem=stat_recv.at[plane],
            device_id=(target * slab + lax.rem(lat_pos, slab), lon_pos),
            device_id_type=MESH,
        )

    def is_self(level):
        return jnp.logical_and(level == lat_pos, plane == lon_pos)

    for i in range(slab):
        level = plane * slab + i

        @pl.when(is_self(level))
        def _():
            pltpu.make_async_copy(send.at[level], recv.at[here], recv_sem.at[here]).start()

        @pl.when(jnp.logical_not(is_self(level)))
        def _():
            remote(level).start()

    def pass_from_below():
        pl.semaphore_wait(from_below, 1)
        call_above(from_below)

    def pass_from_above():
        pl.semaphore_wait(from_above, 1)
        call_below(from_above)

    def post_plane(target):
        for i in range(slab):
            remote(target * slab + i).start()

    def loop(low, high, body):
        def step(n, carry):
            body(n)
            return carry

        lax.fori_loop(low, high, step, 0)

    lower = plane < planes // 2

    @pl.when(lower)
    def _():
        loop(0, plane, lambda n: pass_from_below())
        loop(0, plane, lambda n: tell(n).start())

        def up(n):
            pass_from_above()
            tell(n).start()
            post_plane(n)

        loop(plane + 1, planes, up)
        loop(0, plane, post_plane)

    @pl.when(jnp.logical_not(lower))
    def _():
        loop(plane + 1, planes, lambda n: pass_from_above())
        loop(0, plane, lambda n: pass_from_below())
        loop(0, plane, lambda n: tell(n).start())
        loop(plane + 1, planes, lambda n: tell(n).start())
        loop(0, plane, post_plane)
        loop(plane + 1, planes, post_plane)

    def others(n, body):
        @pl.when(n != plane)
        def _():
            body(n)

    loop(0, planes, lambda n: others(n, lambda m: pltpu.make_async_copy(
        first_stats.at[m], first_stats.at[m], stat_recv.at[m]).wait()))
    last_stats[here] = jnp.max(first_stats[...], axis=0)

    def share(step):
        other = lax.rem(here + step, plane_size)
        return pltpu.make_async_remote_copy(
            src_ref=last_stats.at[here],
            dst_ref=last_stats.at[here],
            send_sem=last_send.at[step],
            recv_sem=last_recv.at[step],
            device_id=(plane * slab + other // lon_count, lax.rem(other, lon_count)),
            device_id_type=MESH,
        )

    loop(1, plane_size, lambda n: share(n).start())

    per_field = (slab * rows) * lon_count

    for b in range(lon_count):
        for i in range(slab):
            source = i * lon_count + b
            pltpu.make_async_copy(recv.at[source], recv.at[source], recv_sem.at[source]).wait()
            stage[source] = recv[source]
            rank = jnp.int32(0)
            for r in range(rows):
                live = mask[b, (lon_pos * slab + i) * rows + r]
                strip = stage[source, jnp.minimum(rank, slots - 1)]
                strip = jnp.where(live > 0, strip, 0.0)
                line = i * rows + r
                start = (line // 8 * lon_count + b) * 8 + line % 8
                out[pl.ds(start, fields, stride=per_field), :] = strip
                rank = rank + live

    loop(1, plane_size, lambda n: share(n).wait())
    for end in range(2):
        first = (end * levels + lat_pos) * fields
        best = jnp.max(last_stats[:, first // STRIP], axis=0)
        best = jnp.broadcast_to(best, (8, STRIP))
        own = pltpu.roll(best, lax.rem(STRIP - lax.rem(first, STRIP), STRIP), 1)
        own = own[:1, :fields]
        rng[end] = own if end == 0 else -own

    def drain(level, carry):
        @pl.when(jnp.logical_not(is_self(level)))
        def _():
            remote(level).wait_send()

        return carry

    lax.fori_loop(0, lat_count, drain, 0)
    loop(0, planes, lambda n: others(n, lambda m: tell(m).wait_send()))


def per_device(fields, ocean_mask, scale_table, offset_table, scale_index, offset_index):
    nfield, levels, rows, cells = fields.shape
    lat_count = lax.axis_size("lat")
    lon_count = lax.axis_size("lon")
    slab = lat_count // lon_count
    slots = min(MAX_LIVE, rows)
    sources = slab * lon_count
    out_rows = nfield * slab * rows * lon_count
    hbm = pl.BlockSpec(memory_space=pltpu.HBM)
    stat_rows = 2 * levels * nfield // STRIP
    vmem = pl.BlockSpec(memory_space=pltpu.VMEM)
    history, record_range = pl.pallas_call(
        functools.partial(kernel, (nfield, levels, rows, lat_count, lon_count)),
        out_shape=(
            jax.ShapeDtypeStruct((out_rows, STRIP), jnp.float32),
            jax.ShapeDtypeStruct((2, 1, nfield), jnp.float32),
        ),
        in_specs=[hbm] * 6,
        out_specs=(vmem, vmem),
        scratch_shapes=[
            pltpu.SMEM((lon_count, lat_count * rows), jnp.int32),
            pltpu.SMEM(scale_table.shape, jnp.float32),
            pltpu.SMEM(offset_table.shape, jnp.float32),
            pltpu.SMEM(scale_index.shape, jnp.int32),
            pltpu.SMEM(offset_index.shape, jnp.int32),
            pltpu.VMEM((nfield * levels * rows, STRIP), jnp.float32),
            pltpu.VMEM((levels, slots, nfield, STRIP), jnp.float32),
            pltpu.VMEM((sources, slots, nfield, STRIP), jnp.float32),
            pltpu.VMEM((sources, slots, nfield, STRIP), jnp.float32),
            pltpu.VMEM((2 * levels * nfield, STRIP), jnp.float32),
            pltpu.VMEM((lat_count // slab, stat_rows, 1, STRIP), jnp.float32),
            pltpu.VMEM((sources, stat_rows, 1, STRIP), jnp.float32),
            pltpu.SemaphoreType.DMA((6,)),
            pltpu.SemaphoreType.DMA((levels,)),
            pltpu.SemaphoreType.DMA((sources,)),
            pltpu.SemaphoreType.DMA((lat_count // slab,)),
            pltpu.SemaphoreType.DMA((lat_count // slab,)),
            pltpu.SemaphoreType.DMA((sources,)),
            pltpu.SemaphoreType.DMA((sources,)),
            pltpu.SemaphoreType.REGULAR,
            pltpu.SemaphoreType.REGULAR,
        ],
        compiler_params=pltpu.CompilerParams(
            collective_id=0, has_side_effects=True
        ),
    )(
        ocean_mask.T, scale_table, offset_table, scale_index, offset_index,
        fields.reshape(nfield * levels * rows, cells),
    )
    history = history.reshape(nfield, slab * rows // 8, lon_count, 8, STRIP)
    history = history.transpose(0, 1, 3, 2, 4)
    return history.reshape(nfield, 1, slab * rows, lon_count * STRIP), record_range.reshape(2, nfield, 1)


def solution(mesh):
    return jax.shard_map(
        per_device,
        mesh=mesh,
        in_specs=(P(None, None, "lat", "lon"), P(), P(), P(), P(), P()),
        out_specs=(P(None, "lat", "lon", None), P(None, None, "lat")),
        check_vma=False,
    )
```

profile of v0, /device:TPU:25, one launch (start us, length us, event | category | flops | bytes accessed | tf_op | source)
XLA Modules:
  0.0 20.0 jit_solution(6042078273437146195)
XLA Ops:
  0.6 16.9 %shard_map.77 = (f32[1024,128]{1,0:T(8,128)}, f32[2,1,8]{2,1,0:T(1,128)}) custom-call(s32[4,128]{1,0:T(4,128)} %bitcast.12, f32[16]{0:T(128)} %scale_table_hbm.1, f32[16]{0:T(128)} %offset_table_hbm.1, s32[8]{0:T(128)} %scale_index_hbm.1, s32[8]{0:T(128)} %offset_index_hbm.1, f32[1024,128]{1,0:T(8,128)} %bitcast.10), custom_call_target="tpu_custom_call" | custom-call | tf_op jit(solution)/shard_map/pallas_call | solution.py:263
  17.5 0.0 copy-start
  17.5 1.9 %copy.11 = f32[8,1,32,512]{3,2,1,0:T(8,128)} copy(f32[8,1,32,512]{3,2,1,0:T(8,128)} %bitcast.11) | data formatting | bytes 1048576
  19.4 0.0 copy-done
  19.4 0.6 %copy.12 = f32[2,8,1]{1,2,0:T(1,128)} copy(f32[2,8,1]{1,2,0:T(1,128)S(1)} %bitcast.13) | data formatting | bytes 128
Async XLA Ops:
  17.5 1.9 %copy-start = (f32[2,1,8]{2,1,0:T(1,128)S(1)}, f32[2,1,8]{2,1,0:T(1,128)}, u32[]{:S(2)}) copy-start(f32[2,1,8]{2,1,0:T(1,128)} %get-tuple-element.5) | copy-start | bytes 196
where the time goes:
time: 20.1 us; the launch traced here: 20 us
  Pallas kernels  16.9 us (84%)
  local copies, waits for them, and re-layouts  2.44 us (12%)
  between operations  0.65 us (3%)
    pallas_call x1, Pallas kernels, per_device(): pl.pallas_call(functools.partial(kernel, (nfield, levels, rows, lat_count...  16.9 us
    unnamed x4, local copies, waits for them, and re-layouts  2.44 us

commit v1 on v0

v1 whole, which is shorter than its diff:
```python
import functools

import jax
import jax.numpy as jnp
from jax import lax
from jax.experimental import pallas as pl
from jax.experimental.pallas import tpu as pltpu
from jax.sharding import PartitionSpec as P

STRIP = 128
MAX_LIVE = 12
MESH = pl.DeviceIdType.MESH


def loop(low, high, body):
    def step(n, carry):
        body(n)
        return carry

    lax.fori_loop(low, high, step, 0)


def exchange(
    dims, mask_hbm, scale_table_hbm, offset_table_hbm, scale_index_hbm, offset_index_hbm, x_hbm,
    out, rng, *scratch,
):
    fields, levels, rows, lat_count, lon_count = dims
    xs, (
        mask, scale_table, offset_table, scale_index, offset_index,
        send, recv, stage, part, mine, first_stats, last_stats,
        x_sem, in_sem, send_sem, recv_sem, stat_send, stat_recv, last_send, last_recv,
    ) = scratch[:levels], scratch[levels:]
    slab = lat_count // lon_count
    planes = lat_count // slab
    sources = slab * lon_count
    slots = send.shape[1]
    lat_pos = lax.axis_index("lat")
    lon_pos = lax.axis_index("lon")
    plane = lat_pos // slab
    here = lax.rem(lat_pos, slab) * lon_count + lon_pos
    lower = plane < planes // 2
    home = plane == lon_pos

    def order(n):
        block, i = n // slab, n % slab
        up = lax.rem(plane + 1 + block, planes)
        down = jnp.where(block < plane, block, jnp.where(block + 1 < planes, block + 1, plane))
        return jnp.where(lower, up, down) * slab + lax.rem(lat_pos + i, slab)

    levels_in_order = [order(n) for n in range(levels)]

    barrier = pltpu.get_barrier_semaphore()

    def greet(source):
        lat, lon = lon_pos * slab + source // lon_count, lax.rem(source, lon_count)

        @pl.when(jnp.logical_not(jnp.logical_and(lat == lat_pos, lon == lon_pos)))
        def _():
            pl.semaphore_signal(barrier, inc=1, device_id=(lat, lon), device_id_type=MESH)

    def greet_lon(step):
        pl.semaphore_signal(
            barrier, inc=1, device_id=(lat_pos, lax.rem(lon_pos + step, lon_count)), device_id_type=MESH
        )

    smalls = [
        pltpu.make_async_copy(src, dst, in_sem.at[n])
        for n, (src, dst) in enumerate([
            (mask_hbm, mask), (scale_table_hbm, scale_table), (offset_table_hbm, offset_table),
            (scale_index_hbm, scale_index), (offset_index_hbm, offset_index),
        ])
    ]
    loads = [
        pltpu.make_async_copy(x_hbm.at[:, levels_in_order[n]], xs[n], x_sem.at[n]) for n in range(levels)
    ]
    loop(0, sources, greet)
    for copy in smalls:
        copy.start()
    for copy in loads:
        copy.start()
    loop(1, lon_count, greet_lon)
    for copy in smalls:
        copy.wait()

    seen = []
    total = jnp.int32(0)
    for r in range(rows):
        total = total + mask[lon_pos, lat_pos * rows + r]
        seen.append(total)
    picks = []
    for k in range(slots):
        slot = jnp.minimum(k, total - 1)
        pick = jnp.int32(0)
        for r in range(rows - 1):
            pick = pick + (seen[r] <= slot).astype(jnp.int32)
        picks.append(pick)

    which = lax.broadcasted_iota(jnp.int32, (fields, STRIP), 0)
    scales = jnp.zeros((fields, STRIP), jnp.float32)
    offsets = jnp.zeros((fields, STRIP), jnp.float32)
    for f in range(fields):
        scales = jnp.where(which == f, scale_table[scale_index[f]], scales)
        offsets = jnp.where(which == f, offset_table[offset_index[f]], offsets)

    for n in range(levels):
        loads[n].wait()
        lines = xs[n].reshape(fields * rows, STRIP)
        high = None
        for k in range(slots):
            strip = lines[pl.ds(picks[k], fields, stride=rows), :]
            packed = (strip - offsets) * scales
            send[n, k] = packed
            high = packed if k == 0 else jnp.maximum(high, packed)
            low = -packed if k == 0 else jnp.maximum(low, -packed)
        level = levels_in_order[n]
        part[pl.ds(pl.multiple_of(level * fields, fields), fields), :] = high
        part[pl.ds(pl.multiple_of((levels + level) * fields, fields), fields), :] = low

    for j in range(mine.shape[0]):
        tile = part[j * STRIP:(j + 1) * STRIP, :].T
        mine[j] = jnp.max(tile, axis=0, keepdims=True)

    pl.semaphore_wait(barrier, levels + lon_count - 1 - home.astype(jnp.int32))

    def is_self(level):
        return jnp.logical_and(level == lat_pos, home)

    def tell(level):
        return pltpu.make_async_remote_copy(
            src_ref=mine,
            dst_ref=first_stats.at[here],
            send_sem=stat_send.at[level],
            recv_sem=stat_recv.at[here],
            device_id=(level, plane),
            device_id_type=MESH,
        )

    def remote(n):
        return pltpu.make_async_remote_copy(
            src_ref=send.at[n],
            dst_ref=recv.at[here],
            send_sem=send_sem.at[n],
            recv_sem=recv_sem.at[here],
            device_id=(levels_in_order[n], plane),
            device_id_type=MESH,
        )

    def when_remote(level, body):
        pl.when(jnp.logical_not(is_self(level)))(body)

    loop(0, levels, lambda level: when_remote(level, lambda: tell(level).start()))
    for n in range(levels):
        when_remote(levels_in_order[n], lambda n=n: remote(n).start())

    @pl.when(home)
    def _():
        first_stats[here] = mine[...]

    for n in range(levels - slab, levels):

        @pl.when(is_self(levels_in_order[n]))
        def _(n=n):
            recv[here] = send[n]

    def not_me(source, body):
        pl.when(jnp.logical_not(jnp.logical_and(home, source == here)))(body)

    loop(0, sources, lambda source: not_me(source, lambda: pltpu.make_async_copy(
        first_stats.at[source], first_stats.at[source], stat_recv.at[source]).wait()))
    last_stats[lon_pos] = jnp.max(first_stats[...], axis=0)

    def share(step):
        return pltpu.make_async_remote_copy(
            src_ref=last_stats.at[lon_pos],
            dst_ref=last_stats.at[lon_pos],
            send_sem=last_send.at[step],
            recv_sem=last_recv.at[step],
            device_id=(lat_pos, lax.rem(lon_pos + step, lon_count)),
            device_id_type=MESH,
        )

    loop(1, lon_count, lambda n: share(n).start())

    per_field = (slab * rows) * lon_count

    for b in range(lon_count):
        for i in range(slab):
            source = i * lon_count + b
            not_me(source, lambda source=source: pltpu.make_async_copy(
                recv.at[source], recv.at[source], recv_sem.at[source]).wait())
            stage[source] = recv[source]
            rank = jnp.int32(0)
            for r in range(rows):
                live = mask[b, (lon_pos * slab + i) * rows + r]
                strip = stage[source, jnp.minimum(rank, slots - 1)]
                strip = jnp.where(live > 0, strip, 0.0)
                line = i * rows + r
                start = (line // 8 * lon_count + b) * 8 + line % 8
                out[pl.ds(start, fields, stride=per_field), :] = strip
                rank = rank + live

    loop(1, lon_count, lambda n: share(n).wait())
    for end in range(2):
        first = (end * levels + lat_pos) * fields
        best = jnp.max(last_stats[:, first // STRIP], axis=0)
        best = jnp.broadcast_to(best, (8, STRIP))
        own = pltpu.roll(best, lax.rem(STRIP - lax.rem(first, STRIP), STRIP), 1)
        own = own[:1, :fields]
        rng[end] = own if end == 0 else -own

    for n in range(levels):
        when_remote(levels_in_order[n], lambda n=n: remote(n).wait_send())
    loop(0, levels, lambda level: when_remote(level, lambda: tell(level).wait_send()))


def store(history, record_range, history_out, record_range_out, sem):
    copies = [
        pltpu.make_async_copy(history, history_out, sem.at[0]),
        pltpu.make_async_copy(record_range, record_range_out, sem.at[1]),
    ]
    for copy in copies:
        copy.start()
    for copy in copies:
        copy.wait()


def per_device(fields, ocean_mask, scale_table, offset_table, scale_index, offset_index):
    nfield, levels, rows, cells = fields.shape
    lat_count = lax.axis_size("lat")
    lon_count = lax.axis_size("lon")
    slab = lat_count // lon_count
    slots = min(MAX_LIVE, rows)
    sources = slab * lon_count
    out_rows = nfield * slab * rows * lon_count
    stat_rows = 2 * levels * nfield // STRIP
    hbm = pl.BlockSpec(memory_space=pltpu.HBM)
    vmem = pl.BlockSpec(memory_space=pltpu.VMEM)
    history, record_range = pl.pallas_call(
        functools.partial(exchange, (nfield, levels, rows, lat_count, lon_count)),
        out_shape=(
            pltpu.VMEM((out_rows, STRIP), jnp.float32),
            pltpu.VMEM((2, 1, nfield), jnp.float32),
        ),
        in_specs=[hbm] * 6,
        out_specs=(vmem, vmem),
        scratch_shapes=[pltpu.VMEM((nfield, rows, STRIP), jnp.float32)] * levels + [
            pltpu.SMEM((lon_count, lat_count * rows), jnp.int32),
            pltpu.SMEM(scale_table.shape, jnp.float32),
            pltpu.SMEM(offset_table.shape, jnp.float32),
            pltpu.SMEM(scale_index.shape, jnp.int32),
            pltpu.SMEM(offset_index.shape, jnp.int32),
            pltpu.VMEM((levels, slots, nfield, STRIP), jnp.float32),
            pltpu.VMEM((sources, slots, nfield, STRIP), jnp.float32),
            pltpu.VMEM((sources, slots, nfield, STRIP), jnp.float32),
            pltpu.VMEM((2 * levels * nfield, STRIP), jnp.float32),
            pltpu.VMEM((stat_rows, 1, STRIP), jnp.float32),
            pltpu.VMEM((sources, stat_rows, 1, STRIP), jnp.float32),
            pltpu.VMEM((lon_count, stat_rows, 1, STRIP), jnp.float32),
            pltpu.SemaphoreType.DMA((levels,)),
            pltpu.SemaphoreType.DMA((5,)),
            pltpu.SemaphoreType.DMA((levels,)),
            pltpu.SemaphoreType.DMA((sources,)),
            pltpu.SemaphoreType.DMA((levels,)),
            pltpu.SemaphoreType.DMA((sources,)),
            pltpu.SemaphoreType.DMA((lon_count,)),
            pltpu.SemaphoreType.DMA((lon_count,)),
        ],
        compiler_params=pltpu.CompilerParams(
            collective_id=0, has_side_effects=True
        ),
    )(ocean_mask.T, scale_table, offset_table, scale_index, offset_index, fields)
    history, record_range = pl.pallas_call(
        store,
        out_shape=(
            jax.ShapeDtypeStruct(history.shape, jnp.float32),
            jax.ShapeDtypeStruct(record_range.shape, jnp.float32),
        ),
        in_specs=[vmem, vmem],
        out_specs=(hbm, hbm),
        scratch_shapes=[pltpu.SemaphoreType.DMA((2,))],
        compiler_params=pltpu.CompilerParams(vmem_limit_bytes=1 << 20),
    )(
        pltpu.with_memory_space_constraint(history, pltpu.VMEM),
        pltpu.with_memory_space_constraint(record_range, pltpu.VMEM),
    )
    history = history.reshape(nfield, slab * rows // 8, lon_count, 8, STRIP)
    history = history.transpose(0, 1, 3, 2, 4)
    return history.reshape(nfield, 1, slab * rows, lon_count * STRIP), record_range.reshape(2, nfield, 1)


def solution(mesh):
    return jax.shard_map(
        per_device,
        mesh=mesh,
        in_specs=(P(None, None, "lat", "lon"), P(), P(), P(), P(), P()),
        out_specs=(P(None, "lat", "lon", None), P(None, None, "lat")),
        check_vma=False,
    )
```

time: 20.1 us -> 17.9 us (0.89)
  the two profiles are of different devices: /device:TPU:25 before, /device:TPU:0 now
where the time goes in v1:
time: 17.9 us; the launch traced here: 17.7 us
  Pallas kernels  17.1 us (96%)
  between operations  0.64 us (4%)
    pallas_call x1, Pallas kernels, per_device(): pl.pallas_call(functools.partial(exchange, (nfield, levels, rows, lat_cou...  16.3 us
    pallas_call x1, Pallas kernels, per_device(): pl.pallas_call(store, out_shape=(jax.ShapeDtypeStruct(history.shape, jnp....  0.81 us

profile of v1, /device:TPU:0, one launch (start us, length us, event | category | flops | bytes accessed | tf_op | source)
XLA Modules:
  0.0 17.7 jit_solution(2625748648349211819)
XLA Ops:
  0.6 16.3 %shard_map.77 = (f32[1024,128]{1,0:T(8,128)S(1)}, f32[2,1,8]{2,1,0:T(1,128)S(1)}) custom-call(s32[4,128]{1,0:T(4,128)} %bitcast.9, f32[16]{0:T(128)} %scale_table_hbm.1, f32[16]{0:T(128)} %offset_table_hbm.1, s32[8]{0:T(128)} %scale_index_hbm.1, s32[8]{0:T(128)} %offset_index_hbm.1, f32[8,8,16,128]{3,2,1,0:T(8,128)} %x_hbm.1), custom_call_target="tpu_custom_call" | custom-call | tf_op jit(solution)/shard_map/pallas_call | solution.py:238
  16.9 0.8 %shard_map.78 = (f32[1024,128]{1,0:T(8,128)}, f32[2,1,8]{2,1,0:T(1,128)}) custom-call(f32[1024,128]{1,0:T(8,128)S(1)} %get-tuple-element.6.history, f32[2,1,8]{2,1,0:T(1,128)S(1)} %get-tuple-element.7.record_range), custom_call_target="tpu_custom_call" | custom-call | tf_op jit(solution)/shard_map/pallas_call | solution.py:272

commit v2 on v1

--- a/solution.py
+++ b/solution.py
@@ -28,7 +28,7 @@
     xs, (
         mask, scale_table, offset_table, scale_index, offset_index,
         send, recv, stage, part, mine, first_stats, last_stats,
-        x_sem, in_sem, send_sem, recv_sem, stat_send, stat_recv, last_send, last_recv,
+        x_sem, in_sem, send_sem, recv_sem, stat_send, stat_recv, last_send, last_recv, token,
     ) = scratch[:levels], scratch[levels:]
     slab = lat_count // lon_count
     planes = lat_count // slab
@@ -40,25 +40,29 @@
     here = lax.rem(lat_pos, slab) * lon_count + lon_pos
     lower = plane < planes // 2
     home = plane == lon_pos
+    last = planes - 1
+    late_core = lax.rem(lon_pos, 2) == 0
+    partner = lon_pos + 1 - 2 * lax.rem(lon_pos, 2)
 
     def order(n):
-        block, i = n // slab, n % slab
-        up = lax.rem(plane + 1 + block, planes)
-        down = jnp.where(block < plane, block, jnp.where(block + 1 < planes, block + 1, plane))
-        return jnp.where(lower, up, down) * slab + lax.rem(lat_pos + i, slab)
+        block, i = n // slab, lax.rem(n, slab)
+        early = jnp.where(lower, last - 1 - block, block)
+        return jnp.where(block < last, early, last) * slab + lax.rem(lat_pos + i, slab)
 
     levels_in_order = [order(n) for n in range(levels)]
 
     barrier = pltpu.get_barrier_semaphore()
-
-    def greet(source):
-        lat, lon = lon_pos * slab + source // lon_count, lax.rem(source, lon_count)
-
-        @pl.when(jnp.logical_not(jnp.logical_and(lat == lat_pos, lon == lon_pos)))
-        def _():
-            pl.semaphore_signal(barrier, inc=1, device_id=(lat, lon), device_id_type=MESH)
-
-    def greet_lon(step):
+    to_late = (plane == last).astype(jnp.int32)
+
+    for i in range(slab):
+        for j in range(lon_count // 2):
+            lat, lon = lon_pos * slab + i, 2 * j + 1 - to_late
+
+            @pl.when(jnp.logical_not(jnp.logical_and(lat == lat_pos, lon == lon_pos)))
+            def _(lat=lat, lon=lon):
+                pl.semaphore_signal(barrier, inc=1, device_id=(lat, lon), device_id_type=MESH)
+
+    for step in range(1, lon_count):
         pl.semaphore_signal(
             barrier, inc=1, device_id=(lat_pos, lax.rem(lon_pos + step, lon_count)), device_id_type=MESH
         )
@@ -73,12 +77,10 @@
     loads = [
         pltpu.make_async_copy(x_hbm.at[:, levels_in_order[n]], xs[n], x_sem.at[n]) for n in range(levels)
     ]
-    loop(0, sources, greet)
     for copy in smalls:
         copy.start()
     for copy in loads:
         copy.start()
-    loop(1, lon_count, greet_lon)
     for copy in smalls:
         copy.wait()
 
@@ -120,18 +122,23 @@
         tile = part[j * STRIP:(j + 1) * STRIP, :].T
         mine[j] = jnp.max(tile, axis=0, keepdims=True)
 
-    pl.semaphore_wait(barrier, levels + lon_count - 1 - home.astype(jnp.int32))
+    self_late = jnp.logical_and(home, plane == last)
+    count_late = slab - self_late.astype(jnp.int32)
+    self_early = jnp.logical_and(home, plane != last)
+    count_early = levels - slab - self_early.astype(jnp.int32)
+    pl.semaphore_wait(barrier, jnp.where(late_core, count_late, count_early) + lon_count - 1)
+    pl.semaphore_signal(token, inc=1, device_id=(lat_pos, partner), device_id_type=MESH)
 
     def is_self(level):
         return jnp.logical_and(level == lat_pos, home)
 
-    def tell(level):
+    def tell(n):
         return pltpu.make_async_remote_copy(
             src_ref=mine,
             dst_ref=first_stats.at[here],
-            send_sem=stat_send.at[level],
+            send_sem=stat_send.at[n],
             recv_sem=stat_recv.at[here],
-            device_id=(level, plane),
+            device_id=(order(n), plane),
             device_id_type=MESH,
         )
 
@@ -141,26 +148,36 @@
             dst_ref=recv.at[here],
             send_sem=send_sem.at[n],
             recv_sem=recv_sem.at[here],
-            device_id=(levels_in_order[n], plane),
+            device_id=(order(n), plane),
             device_id_type=MESH,
         )
 
-    def when_remote(level, body):
-        pl.when(jnp.logical_not(is_self(level)))(body)
-
-    loop(0, levels, lambda level: when_remote(level, lambda: tell(level).start()))
-    for n in range(levels):
-        when_remote(levels_in_order[n], lambda n=n: remote(n).start())
+    def when_remote(n, body):
+        pl.when(jnp.logical_not(is_self(order(n))))(body)
+
+    def post(first, end):
+        loop(first, end, lambda n: when_remote(n, lambda: tell(n).start()))
+        loop(first, end, lambda n: when_remote(n, lambda: remote(n).start()))
+
+    @pl.when(late_core)
+    def _():
+        pl.semaphore_wait(token, 1)
+        loop(0, levels, lambda n: when_remote(n, lambda: tell(n).start()))
+        shift = jnp.where(lower, levels - slab, 0)
+        loop(shift, levels, lambda n: when_remote(n, lambda: remote(n).start()))
+        loop(0, shift, lambda n: when_remote(n, lambda: remote(n).start()))
+
+    @pl.when(jnp.logical_not(late_core))
+    def _():
+        post(0, levels - slab)
+        pl.semaphore_wait(token, 1)
+        post(levels - slab, levels)
 
     @pl.when(home)
     def _():
         first_stats[here] = mine[...]
-
-    for n in range(levels - slab, levels):
-
-        @pl.when(is_self(levels_in_order[n]))
-        def _(n=n):
-            recv[here] = send[n]
+        block = jnp.where(jnp.logical_and(lower, plane < last), last - 1 - plane, plane)
+        recv[here] = send[block * slab]
 
     def not_me(source, body):
         pl.when(jnp.logical_not(jnp.logical_and(home, source == here)))(body)
@@ -208,9 +225,8 @@
         own = own[:1, :fields]
         rng[end] = own if end == 0 else -own
 
-    for n in range(levels):
-        when_remote(levels_in_order[n], lambda n=n: remote(n).wait_send())
-    loop(0, levels, lambda level: when_remote(level, lambda: tell(level).wait_send()))
+    loop(0, levels, lambda n: when_remote(n, lambda: remote(n).wait_send()))
+    loop(0, levels, lambda n: when_remote(n, lambda: tell(n).wait_send()))
 
 
 def store(history, record_range, history_out, record_range_out, sem):
@@ -264,6 +280,7 @@
             pltpu.SemaphoreType.DMA((sources,)),
             pltpu.SemaphoreType.DMA((lon_count,)),
             pltpu.SemaphoreType.DMA((lon_count,)),
+            pltpu.SemaphoreType.REGULAR,
         ],
         compiler_params=pltpu.CompilerParams(
             collective_id=0, has_side_effects=True

time: 17.9 us -> 17.7 us (0.989)
  Pallas kernels: 17.1 us -> 16.9 us
where the time goes in v2:
time: 17.7 us; the launch traced here: 17.6 us
  Pallas kernels  16.9 us (95%)
  between operations  0.64 us (4%)
    pallas_call x1, Pallas kernels, per_device(): pl.pallas_call(functools.partial(exchange, (nfield, levels, rows, lat_cou...  16.1 us
    pallas_call x1, Pallas kernels, per_device(): pl.pallas_call(store, out_shape=(jax.ShapeDtypeStruct(history.shape, jnp....  0.81 us

profile of v2, /device:TPU:0, one launch (start us, length us, event | category | flops | bytes accessed | tf_op | source)
XLA Modules:
  0.0 17.6 jit_solution(13011139693403125043)
XLA Ops:
  0.6 16.1 %shard_map.77 = (f32[1024,128]{1,0:T(8,128)S(1)}, f32[2,1,8]{2,1,0:T(1,128)S(1)}) custom-call(s32[4,128]{1,0:T(4,128)} %bitcast.9, f32[16]{0:T(128)} %scale_table_hbm.1, f32[16]{0:T(128)} %offset_table_hbm.1, s32[8]{0:T(128)} %scale_index_hbm.1, s32[8]{0:T(128)} %offset_index_hbm.1, f32[8,8,16,128]{3,2,1,0:T(8,128)} %x_hbm.1), custom_call_target="tpu_custom_call" | custom-call | tf_op jit(solution)/shard_map/pallas_call | solution.py:254
  16.8 0.8 %shard_map.78 = (f32[1024,128]{1,0:T(8,128)}, f32[2,1,8]{2,1,0:T(1,128)}) custom-call(f32[1024,128]{1,0:T(8,128)S(1)} %get-tuple-element.6.history, f32[2,1,8]{2,1,0:T(1,128)S(1)} %get-tuple-element.7.record_range), custom_call_target="tpu_custom_call" | custom-call | tf_op jit(solution)/shard_map/pallas_call | solution.py:289

commit v3 on v2

v3 whole, which is shorter than its diff:
```python
import functools

import jax
import jax.numpy as jnp
from jax import lax
from jax.experimental import pallas as pl
from jax.experimental.pallas import tpu as pltpu
from jax.sharding import PartitionSpec as P

STRIP = 128
MAX_LIVE = 12
MESH = pl.DeviceIdType.MESH


def loop(low, high, body):
    def step(n, carry):
        body(n)
        return carry

    lax.fori_loop(low, high, step, 0)


def unless(condition, body):
    pl.when(jnp.logical_not(condition))(body)


def exchange(
    dims, mask_hbm, scale_table_hbm, offset_table_hbm, scale_index_hbm, offset_index_hbm, x_hbm,
    out, rng,
    mask, scale_table, offset_table, scale_index, offset_index,
    xs, send, recv, stage, part, mine, first_stats, last_stats,
    x_sem, in_sem, send_sem, recv_sem, stat_send, stat_recv, last_send, last_recv, token,
):
    fields, levels, rows, lat_count, lon_count = dims
    slab = lat_count // lon_count
    planes = lat_count // slab
    sources = slab * lon_count
    slots = send.shape[1]
    last = planes - 1
    lat_pos = lax.axis_index("lat")
    lon_pos = lax.axis_index("lon")
    plane = lat_pos // slab
    here = lax.rem(lat_pos, slab) * lon_count + lon_pos
    lower = plane < planes // 2
    home = plane == lon_pos
    partner = lon_pos + 1 - 2 * lax.rem(lon_pos, 2)
    collects = jnp.logical_and(home, lax.rem(lat_pos, slab) == slab - 1)

    def order(n):
        block, i = n // slab, lax.rem(n, slab)
        early = jnp.where(lower, last - 1 - block, block)
        return jnp.where(block < last, early, last) * slab + lax.rem(lat_pos + 1 + i, slab)

    barrier = pltpu.get_barrier_semaphore()

    def signal(sem, lat, lon):
        pl.semaphore_signal(sem, inc=1, device_id=(lat, lon), device_id_type=MESH)

    @pl.when(plane != last)
    def _():
        for i in range(slab):
            for b in range(lon_count):
                lat = lon_pos * slab + i
                itself = jnp.logical_and(lat == lat_pos, b == lon_pos)
                skip = jnp.logical_or(itself, b == lon_pos) if i == slab - 1 else itself
                unless(skip, lambda lat=lat, b=b: signal(barrier, lat, b))

    unless(jnp.logical_or(plane != last, collects), lambda: signal(barrier, lon_pos * slab + slab - 1, lon_pos))
    for step in range(1, lon_count):
        signal(barrier, lat_pos, lax.rem(lon_pos + step, lon_count))
    unless(collects, lambda: signal(barrier, plane * slab + slab - 1, plane))

    smalls = [
        pltpu.make_async_copy(src, dst, in_sem.at[n])
        for n, (src, dst) in enumerate([
            (mask_hbm, mask), (scale_table_hbm, scale_table), (offset_table_hbm, offset_table),
            (scale_index_hbm, scale_index), (offset_index_hbm, offset_index),
        ])
    ]
    for copy in smalls:
        copy.start()
    for n in range(levels):
        pltpu.make_async_copy(x_hbm.at[:, order(n)], xs.at[n], x_sem).start()
    for copy in smalls:
        copy.wait()

    seen = []
    total = jnp.int32(0)
    for r in range(rows):
        total = total + mask[lon_pos, lat_pos * rows + r]
        seen.append(total)
    picks = []
    for k in range(slots):
        pick = jnp.int32(k)
        for r in range(k, rows - 1):
            pick = pick + (seen[r] <= k).astype(jnp.int32)
        picks.append(pick if k == 0 else jnp.where(k < total, pick, picks[-1]))

    which = lax.broadcasted_iota(jnp.int32, (fields, STRIP), 0)
    scales = jnp.zeros((fields, STRIP), jnp.float32)
    offsets = jnp.zeros((fields, STRIP), jnp.float32)
    for f in range(fields):
        scales = jnp.where(which == f, scale_table[scale_index[f]], scales)
        offsets = jnp.where(which == f, offset_table[offset_index[f]], offsets)

    pltpu.make_async_copy(xs, xs, x_sem).wait()
    lines = xs.reshape(levels * fields * rows, STRIP)
    for n in range(levels):
        high = None
        for k in range(slots):
            strip = lines[pl.ds(n * fields * rows + picks[k], fields, stride=rows), :]
            packed = (strip - offsets) * scales
            send[n, k] = packed
            high = packed if k == 0 else jnp.maximum(high, packed)
            low = -packed if k == 0 else jnp.maximum(low, -packed)
        level = order(n)
        part[pl.ds(pl.multiple_of(level * fields, fields), fields), :] = high
        part[pl.ds(pl.multiple_of((levels + level) * fields, fields), fields), :] = low

    for j in range(mine.shape[0]):
        tile = part[j * STRIP:(j + 1) * STRIP, :].T
        mine[j] = jnp.max(tile, axis=0, keepdims=True)

    own_last = jnp.logical_and(home, plane == last).astype(jnp.int32)
    own_early = jnp.logical_and(home, plane != last).astype(jnp.int32)
    calls = jnp.where(collects, slab - own_last + sources - 1, levels - slab - own_early)
    pl.semaphore_wait(barrier, calls + lon_count - 1)

    @pl.when(collects)
    def _():
        def pass_on(step):
            other = lax.rem(here + step, sources)
            signal(token, plane * slab + other // lon_count, lax.rem(other, lon_count))

        loop(1, sources, pass_on)

    @pl.when(jnp.logical_and(plane == partner, lax.rem(lat_pos, slab) == slab - 1))
    def _():
        signal(token, lat_pos, partner)

    def tell(n):
        return pltpu.make_async_remote_copy(
            src_ref=mine,
            dst_ref=first_stats.at[here],
            send_sem=stat_send,
            recv_sem=stat_recv,
            device_id=(order(n), plane),
            device_id_type=MESH,
        )

    def remote(n):
        return pltpu.make_async_remote_copy(
            src_ref=send.at[n],
            dst_ref=recv.at[here],
            send_sem=send_sem,
            recv_sem=recv_sem.at[here],
            device_id=(order(n), plane),
            device_id_type=MESH,
        )

    def unless_self(n, body):
        unless(jnp.logical_and(order(n) == lat_pos, home), body)

    def post(first, end):
        loop(first, end, lambda n: unless_self(n, lambda: tell(n).start()))
        loop(first, end, lambda n: unless_self(n, lambda: remote(n).start()))

    @pl.when(collects)
    def _():
        pl.semaphore_wait(token, 1)

    post(0, levels - slab)

    @pl.when(jnp.logical_not(collects))
    def _():
        pl.semaphore_wait(token, 1)

    post(levels - slab, levels)

    @pl.when(home)
    def _():
        first_stats[here] = mine[...]
        block = jnp.where(jnp.logical_and(lower, plane < last), last - 1 - plane, plane)
        recv[here] = send[block * slab + slab - 1]

    def wait_all(ref, sem):
        count = ref.shape[0]

        @pl.when(home)
        def _():
            some = ref.at[pl.ds(0, count - 1)]
            pltpu.make_async_copy(some, some, sem).wait()

        unless(home, lambda: pltpu.make_async_copy(ref, ref, sem).wait())

    wait_all(first_stats, stat_recv)
    last_stats[lon_pos] = jnp.max(first_stats[...], axis=0)

    def share(step):
        return pltpu.make_async_remote_copy(
            src_ref=last_stats.at[lon_pos],
            dst_ref=last_stats.at[lon_pos],
            send_sem=last_send,
            recv_sem=last_recv,
            device_id=(lat_pos, lax.rem(lon_pos + step, lon_count)),
            device_id_type=MESH,
        )

    loop(1, lon_count, lambda n: share(n).start())

    def finish_range():
        others = last_stats.at[pl.ds(0, lon_count - 1)]
        pltpu.make_async_copy(others, others, last_recv).wait()
        for end in range(2):
            first = (end * levels + lat_pos) * fields
            best = jnp.max(last_stats[:, first // STRIP], axis=0)
            best = jnp.broadcast_to(best, (8, STRIP))
            own = pltpu.roll(best, lax.rem(STRIP - lax.rem(first, STRIP), STRIP), 1)
            own = own[:1, :fields]
            rng[end] = own if end == 0 else -own

    per_field = (slab * rows) * lon_count

    for turn in range(sources):
        b, i = turn // slab, turn % slab
        source = i * lon_count + b
        if turn == sources - 1:
            finish_range()
        unless(jnp.logical_and(home, source == here), lambda source=source: pltpu.make_async_copy(
            recv.at[source], recv.at[source], recv_sem.at[source]).wait())
        stage[source] = recv[source]
        rank = jnp.int32(0)
        for r in range(rows):
            live = mask[b, (lon_pos * slab + i) * rows + r]
            strip = stage[source, jnp.minimum(rank, slots - 1)]
            strip = jnp.where(live > 0, strip, 0.0)
            line = i * rows + r
            start = (line // 8 * lon_count + b) * 8 + line % 8
            out[pl.ds(start, fields, stride=per_field), :] = strip
            rank = rank + live

    others = last_stats.at[pl.ds(0, lon_count - 1)]
    pltpu.make_async_copy(others, others, last_send).wait()
    wait_all(first_stats, stat_send)
    wait_all(send, send_sem)


def store(history, record_range, history_out, record_range_out, sem):
    copies = [
        pltpu.make_async_copy(history, history_out, sem.at[0]),
        pltpu.make_async_copy(record_range, record_range_out, sem.at[1]),
    ]
    for copy in copies:
        copy.start()
    for copy in copies:
        copy.wait()


def per_device(fields, ocean_mask, scale_table, offset_table, scale_index, offset_index):
    nfield, levels, rows, cells = fields.shape
    lat_count = lax.axis_size("lat")
    lon_count = lax.axis_size("lon")
    slab = lat_count // lon_count
    slots = min(MAX_LIVE, rows)
    sources = slab * lon_count
    out_rows = nfield * slab * rows * lon_count
    stat_rows = 2 * levels * nfield // STRIP
    hbm = pl.BlockSpec(memory_space=pltpu.HBM)
    vmem = pl.BlockSpec(memory_space=pltpu.VMEM)
    history, record_range = pl.pallas_call(
        functools.partial(exchange, (nfield, levels, rows, lat_count, lon_count)),
        out_shape=(
            pltpu.VMEM((out_rows, STRIP), jnp.float32),
            pltpu.VMEM((2, 1, nfield), jnp.float32),
        ),
        in_specs=[hbm] * 6,
        out_specs=(vmem, vmem),
        scratch_shapes=[
            pltpu.SMEM((lon_count, lat_count * rows), jnp.int32),
            pltpu.SMEM(scale_table.shape, jnp.float32),
            pltpu.SMEM(offset_table.shape, jnp.float32),
            pltpu.SMEM(scale_index.shape, jnp.int32),
            pltpu.SMEM(offset_index.shape, jnp.int32),
            pltpu.VMEM((levels, nfield, rows, STRIP), jnp.float32),
            pltpu.VMEM((levels, slots, nfield, STRIP), jnp.float32),
            pltpu.VMEM((sources, slots, nfield, STRIP), jnp.float32),
            pltpu.VMEM((sources, slots, nfield, STRIP), jnp.float32),
            pltpu.VMEM((2 * levels * nfield, STRIP), jnp.float32),
            pltpu.VMEM((stat_rows, 1, STRIP), jnp.float32),
            pltpu.VMEM((sources, stat_rows, 1, STRIP), jnp.float32),
            pltpu.VMEM((lon_count, stat_rows, 1, STRIP), jnp.float32),
            pltpu.SemaphoreType.DMA,
            pltpu.SemaphoreType.DMA((5,)),
            pltpu.SemaphoreType.DMA,
            pltpu.SemaphoreType.DMA((sources,)),
            pltpu.SemaphoreType.DMA,
            pltpu.SemaphoreType.DMA,
            pltpu.SemaphoreType.DMA,
            pltpu.SemaphoreType.DMA,
            pltpu.SemaphoreType.REGULAR,
        ],
        compiler_params=pltpu.CompilerParams(
            collective_id=0, has_side_effects=True
        ),
    )(ocean_mask.T, scale_table, offset_table, scale_index, offset_index, fields)
    history, record_range = pl.pallas_call(
        store,
        out_shape=(
            jax.ShapeDtypeStruct(history.shape, jnp.float32),
            jax.ShapeDtypeStruct(record_range.shape, jnp.float32),
        ),
        in_specs=[vmem, vmem],
        out_specs=(hbm, hbm),
        scratch_shapes=[pltpu.SemaphoreType.DMA((2,))],
        compiler_params=pltpu.CompilerParams(vmem_limit_bytes=1 << 20),
    )(
        pltpu.with_memory_space_constraint(history, pltpu.VMEM),
        pltpu.with_memory_space_constraint(record_range, pltpu.VMEM),
    )
    history = history.reshape(nfield, slab * rows // 8, lon_count, 8, STRIP)
    history = history.transpose(0, 1, 3, 2, 4)
    return history.reshape(nfield, 1, slab * rows, lon_count * STRIP), record_range.reshape(2, nfield, 1)


def solution(mesh):
    return jax.shard_map(
        per_device,
        mesh=mesh,
        in_specs=(P(None, None, "lat", "lon"), P(), P(), P(), P(), P()),
        out_specs=(P(None, "lat", "lon", None), P(None, None, "lat")),
        check_vma=False,
    )
```

time: 17.7 us -> 16.7 us (0.944)
  Pallas kernels: 16.9 us -> 15.9 us
    pallas_call x1, Pallas kernels: 16.1 us -> 15.1 us  [per_device(): pl.pallas_call(functools.partial(exchange, (nfield, levels, rows, lat_cou...]
where the time goes in v3:
time: 16.7 us; the launch traced here: 16.6 us
  Pallas kernels  15.9 us (95%)
  between operations  0.64 us (4%)
    pallas_call x1, Pallas kernels, per_device(): pl.pallas_call(functools.partial(exchange, (nfield, levels, rows, lat_cou...  15.1 us
    pallas_call x1, Pallas kernels, per_device(): pl.pallas_call(store, out_shape=(jax.ShapeDtypeStruct(history.shape, jnp....  0.81 us

profile of v3, /device:TPU:0, one launch (start us, length us, event | category | flops | bytes accessed | tf_op | source)
XLA Modules:
  0.0 16.6 jit_solution(15116823686560446452)
XLA Ops:
  0.6 15.1 %shard_map.77 = (f32[1024,128]{1,0:T(8,128)S(1)}, f32[2,1,8]{2,1,0:T(1,128)S(1)}) custom-call(s32[4,128]{1,0:T(4,128)} %bitcast.9, f32[16]{0:T(128)} %scale_table_hbm.1, f32[16]{0:T(128)} %offset_table_hbm.1, s32[8]{0:T(128)} %scale_index_hbm.1, s32[8]{0:T(128)} %offset_index_hbm.1, f32[8,8,16,128]{3,2,1,0:T(8,128)} %x_hbm.1), custom_call_target="tpu_custom_call" | custom-call | tf_op jit(solution)/shard_map/pallas_call | solution.py:270
  15.8 0.8 %shard_map.78 = (f32[1024,128]{1,0:T(8,128)}, f32[2,1,8]{2,1,0:T(1,128)}) custom-call(f32[1024,128]{1,0:T(8,128)S(1)} %get-tuple-element.6.history, f32[2,1,8]{2,1,0:T(1,128)S(1)} %get-tuple-element.7.record_range), custom_call_target="tpu_custom_call" | custom-call | tf_op jit(solution)/shard_map/pallas_call | solution.py:306

commit v4 on v3

--- a/solution.py
+++ b/solution.py
@@ -28,8 +28,9 @@
     dims, mask_hbm, scale_table_hbm, offset_table_hbm, scale_index_hbm, offset_index_hbm, x_hbm,
     out, rng,
     mask, scale_table, offset_table, scale_index, offset_index,
-    xs, send, recv, stage, part, mine, first_stats, last_stats,
-    x_sem, in_sem, send_sem, recv_sem, stat_send, stat_recv, last_send, last_recv, token,
+    xs, send, recv, stage, part, mine, first_stats, last_stats, best,
+    x_sem, in_sem, send_sem, recv_sem, stat_send, stat_recv, last_send, last_recv, best_send, best_recv,
+    token, cross,
 ):
     fields, levels, rows, lat_count, lon_count = dims
     slab = lat_count // lon_count
@@ -43,13 +44,18 @@
     here = lax.rem(lat_pos, slab) * lon_count + lon_pos
     lower = plane < planes // 2
     home = plane == lon_pos
+    x_pos = lax.rem(lat_pos, slab)
     partner = lon_pos + 1 - 2 * lax.rem(lon_pos, 2)
-    collects = jnp.logical_and(home, lax.rem(lat_pos, slab) == slab - 1)
+    at_end = x_pos == slab - 1
+    collects = jnp.logical_and(home, at_end)
+    helps = jnp.logical_and(plane == partner, at_end)
+
+    def place(block):
+        early = jnp.where(lower, last - 1 - block, block)
+        return jnp.where(block < last, early, last)
 
     def order(n):
-        block, i = n // slab, lax.rem(n, slab)
-        early = jnp.where(lower, last - 1 - block, block)
-        return jnp.where(block < last, early, last) * slab + lax.rem(lat_pos + 1 + i, slab)
+        return place(n // slab) * slab + lax.rem(x_pos + lax.rem(n, slab), slab)
 
     barrier = pltpu.get_barrier_semaphore()
 
@@ -58,17 +64,20 @@
 
     @pl.when(plane != last)
     def _():
-        for i in range(slab):
-            for b in range(lon_count):
-                lat = lon_pos * slab + i
-                itself = jnp.logical_and(lat == lat_pos, b == lon_pos)
-                skip = jnp.logical_or(itself, b == lon_pos) if i == slab - 1 else itself
-                unless(skip, lambda lat=lat, b=b: signal(barrier, lat, b))
-
+        for b in range(lon_count):
+            skip = jnp.logical_and(b == lon_pos, jnp.logical_or(home, at_end))
+            unless(skip, lambda b=b: signal(barrier, lon_pos * slab + x_pos, b))
+
+    for step in range(1, slab):
+        signal(barrier, plane * slab + lax.rem(x_pos + step, slab), lon_pos)
     unless(jnp.logical_or(plane != last, collects), lambda: signal(barrier, lon_pos * slab + slab - 1, lon_pos))
-    for step in range(1, lon_count):
-        signal(barrier, lat_pos, lax.rem(lon_pos + step, lon_count))
     unless(collects, lambda: signal(barrier, plane * slab + slab - 1, plane))
+    pl.when(collects)(lambda: signal(barrier, lat_pos, partner))
+
+    @pl.when(plane != last)
+    def _():
+        for step in range(1, planes):
+            signal(barrier, lax.rem(plane + step, planes) * slab + x_pos, lon_pos)
 
     smalls = [
         pltpu.make_async_copy(src, dst, in_sem.at[n])
@@ -121,10 +130,29 @@
         tile = part[j * STRIP:(j + 1) * STRIP, :].T
         mine[j] = jnp.max(tile, axis=0, keepdims=True)
 
-    own_last = jnp.logical_and(home, plane == last).astype(jnp.int32)
-    own_early = jnp.logical_and(home, plane != last).astype(jnp.int32)
-    calls = jnp.where(collects, slab - own_last + sources - 1, levels - slab - own_early)
-    pl.semaphore_wait(barrier, calls + lon_count - 1)
+    inner = (plane != last).astype(jnp.int32)
+    own = home.astype(jnp.int32)
+    column = planes - 1 - inner
+    calls = jnp.where(
+        collects, slab - own * (1 - inner) + sources - 1, planes - 1 - own * inner + helps.astype(jnp.int32)
+    )
+    pl.semaphore_wait(barrier, column + slab - 1 + calls)
+
+    def row_copy(src, dst, send, receive, lat, lon):
+        return pltpu.make_async_remote_copy(
+            src_ref=src, dst_ref=dst, send_sem=send, recv_sem=receive,
+            device_id=(lat, lon), device_id_type=MESH,
+        )
+
+    def tell(other):
+        return row_copy(
+            mine, first_stats.at[plane], stat_send, stat_recv, other * slab + x_pos, lon_pos
+        )
+
+    def unless_here(other, body):
+        unless(other == plane, body)
+
+    loop(0, last, lambda other: unless_here(other, lambda: tell(other).start()))
 
     @pl.when(collects)
     def _():
@@ -133,20 +161,11 @@
             signal(token, plane * slab + other // lon_count, lax.rem(other, lon_count))
 
         loop(1, sources, pass_on)
-
-    @pl.when(jnp.logical_and(plane == partner, lax.rem(lat_pos, slab) == slab - 1))
-    def _():
-        signal(token, lat_pos, partner)
-
-    def tell(n):
-        return pltpu.make_async_remote_copy(
-            src_ref=mine,
-            dst_ref=first_stats.at[here],
-            send_sem=stat_send,
-            recv_sem=stat_recv,
-            device_id=(order(n), plane),
-            device_id_type=MESH,
-        )
+        pl.semaphore_wait(token, 1)
+
+    pl.when(helps)(lambda: signal(token, lat_pos, partner))
+    for step in range(1, slab):
+        signal(cross, plane * slab + lax.rem(x_pos + step, slab), lon_pos)
 
     def remote(n):
         return pltpu.make_async_remote_copy(
@@ -158,71 +177,75 @@
             device_id_type=MESH,
         )
 
-    def unless_self(n, body):
-        unless(jnp.logical_and(order(n) == lat_pos, home), body)
-
-    def post(first, end):
-        loop(first, end, lambda n: unless_self(n, lambda: tell(n).start()))
-        loop(first, end, lambda n: unless_self(n, lambda: remote(n).start()))
-
-    @pl.when(collects)
+    def post(block, first, end):
+        def start(i):
+            n = block * slab + i
+            unless(jnp.logical_and(order(n) == lat_pos, home), lambda: remote(n).start())
+
+        loop(first, end, start)
+
+    post(0, 0, 1)
+    pl.semaphore_wait(cross, slab - 1)
+    post(0, 1, slab)
+
+    def post_block(block):
+        post(block, 1, slab)
+        post(block, 0, 1)
+
+    loop(1, last, post_block)
+
+    @pl.when(jnp.logical_not(collects))
     def _():
         pl.semaphore_wait(token, 1)
 
-    post(0, levels - slab)
-
-    @pl.when(jnp.logical_not(collects))
-    def _():
-        pl.semaphore_wait(token, 1)
-
-    post(levels - slab, levels)
+    post_block(last)
+    first_stats[plane] = mine[...]
 
     @pl.when(home)
     def _():
-        first_stats[here] = mine[...]
         block = jnp.where(jnp.logical_and(lower, plane < last), last - 1 - plane, plane)
-        recv[here] = send[block * slab + slab - 1]
-
-    def wait_all(ref, sem):
-        count = ref.shape[0]
-
-        @pl.when(home)
+        recv[here] = send[block * slab]
+
+    def wait_rows(ref, count, sem):
+        some = ref.at[pl.ds(0, count)]
+        pltpu.make_async_copy(some, some, sem).wait()
+
+    def share(step):
+        other = lax.rem(here + step, sources)
+        return row_copy(
+            last_stats.at[here], last_stats.at[here], last_send, last_recv,
+            plane * slab + other // lon_count, lax.rem(other, lon_count),
+        )
+
+    @pl.when(plane != last)
+    def _():
+        wait_rows(first_stats, planes - 1, stat_recv)
+        last_stats[here] = jnp.max(first_stats[...], axis=0)
+        loop(1, sources, lambda step: share(step).start())
+
+    forward = row_copy(best, best, best_send, best_recv, last * slab + x_pos, lon_pos)
+
+    def finish_range():
+        @pl.when(plane != last)
         def _():
-            some = ref.at[pl.ds(0, count - 1)]
-            pltpu.make_async_copy(some, some, sem).wait()
-
-        unless(home, lambda: pltpu.make_async_copy(ref, ref, sem).wait())
-
-    wait_all(first_stats, stat_recv)
-    last_stats[lon_pos] = jnp.max(first_stats[...], axis=0)
-
-    def share(step):
-        return pltpu.make_async_remote_copy(
-            src_ref=last_stats.at[lon_pos],
-            dst_ref=last_stats.at[lon_pos],
-            send_sem=last_send,
-            recv_sem=last_recv,
-            device_id=(lat_pos, lax.rem(lon_pos + step, lon_count)),
-            device_id_type=MESH,
-        )
-
-    loop(1, lon_count, lambda n: share(n).start())
-
-    def finish_range():
-        others = last_stats.at[pl.ds(0, lon_count - 1)]
-        pltpu.make_async_copy(others, others, last_recv).wait()
+            wait_rows(last_stats, sources - 1, last_recv)
+            best[...] = jnp.max(last_stats[...], axis=0)
+
+        pl.when(plane == last - 1)(forward.start)
+        pl.when(plane == last)(lambda: pltpu.make_async_copy(best, best, best_recv).wait())
         for end in range(2):
             first = (end * levels + lat_pos) * fields
-            best = jnp.max(last_stats[:, first // STRIP], axis=0)
-            best = jnp.broadcast_to(best, (8, STRIP))
-            own = pltpu.roll(best, lax.rem(STRIP - lax.rem(first, STRIP), STRIP), 1)
-            own = own[:1, :fields]
-            rng[end] = own if end == 0 else -own
+            line = jnp.broadcast_to(best[first // STRIP], (8, STRIP))
+            line = pltpu.roll(line, lax.rem(STRIP - lax.rem(first, STRIP), STRIP), 1)
+            line = line[:1, :fields]
+            rng[end] = line if end == 0 else -line
 
     per_field = (slab * rows) * lon_count
+    pairs = lon_count // 2
 
     for turn in range(sources):
-        b, i = turn // slab, turn % slab
+        core, j, i = 1 - turn // (pairs * slab), turn // slab % pairs, slab - 1 - turn % slab
+        b = 2 * lax.rem(lon_pos // 2 + j, pairs) + core
         source = i * lon_count + b
         if turn == sources - 1:
             finish_range()
@@ -239,10 +262,16 @@
             out[pl.ds(start, fields, stride=per_field), :] = strip
             rank = rank + live
 
-    others = last_stats.at[pl.ds(0, lon_count - 1)]
-    pltpu.make_async_copy(others, others, last_send).wait()
-    wait_all(first_stats, stat_send)
-    wait_all(send, send_sem)
+    pl.when(plane == last - 1)(forward.wait_send)
+
+    @pl.when(plane != last)
+    def _():
+        wait_rows(last_stats, sources - 1, last_send)
+        wait_rows(first_stats, last - 1, stat_send)
+
+    pl.when(plane == last)(lambda: wait_rows(first_stats, last, stat_send))
+    pl.when(home)(lambda: wait_rows(send, levels - 1, send_sem))
+    unless(home, lambda: wait_rows(send, levels, send_sem))
 
 
 def store(history, record_range, history_out, record_range_out, sem):
@@ -287,8 +316,9 @@
             pltpu.VMEM((sources, slots, nfield, STRIP), jnp.float32),
             pltpu.VMEM((2 * levels * nfield, STRIP), jnp.float32),
             pltpu.VMEM((stat_rows, 1, STRIP), jnp.float32),
+            pltpu.VMEM((lat_count // slab, stat_rows, 1, STRIP), jnp.float32),
             pltpu.VMEM((sources, stat_rows, 1, STRIP), jnp.float32),
-            pltpu.VMEM((lon_count, stat_rows, 1, STRIP), jnp.float32),
+            pltpu.VMEM((stat_rows, 1, STRIP), jnp.float32),
             pltpu.SemaphoreType.DMA,
             pltpu.SemaphoreType.DMA((5,)),
             pltpu.SemaphoreType.DMA,
@@ -297,6 +327,9 @@
             pltpu.SemaphoreType.DMA,
             pltpu.SemaphoreType.DMA,
             pltpu.SemaphoreType.DMA,
+            pltpu.SemaphoreType.DMA,
+            pltpu.SemaphoreType.DMA,
+            pltpu.SemaphoreType.REGULAR,
             pltpu.SemaphoreType.REGULAR,
         ],
         compiler_params=pltpu.CompilerParams(

time: 16.7 us -> 15.4 us (0.922)
  the two profiles are of different devices: /device:TPU:0 before, /device:TPU:4 now
where the time goes in v4:
time: 15.4 us; the launch traced here: 15.2 us
  Pallas kernels  14.6 us (95%)
  between operations  0.64 us (4%)
    pallas_call x1, Pallas kernels, per_device(): pl.pallas_call(functools.partial(exchange, (nfield, levels, rows, lat_cou...  13.8 us
    pallas_call x1, Pallas kernels, per_device(): pl.pallas_call(store, out_shape=(jax.ShapeDtypeStruct(history.shape, jnp....  0.81 us

profile of v4, /device:TPU:4, one launch (start us, length us, event | category | flops | bytes accessed | tf_op | source)
XLA Modules:
  0.0 15.2 jit_solution(5655799659221647595)
XLA Ops:
  0.6 13.8 %shard_map.77 = (f32[1024,128]{1,0:T(8,128)S(1)}, f32[2,1,8]{2,1,0:T(1,128)S(1)}) custom-call(s32[4,128]{1,0:T(4,128)} %bitcast.9, f32[16]{0:T(128)} %scale_table_hbm.1, f32[16]{0:T(128)} %offset_table_hbm.1, s32[8]{0:T(128)} %scale_index_hbm.1, s32[8]{0:T(128)} %offset_index_hbm.1, f32[8,8,16,128]{3,2,1,0:T(8,128)} %x_hbm.1), custom_call_target="tpu_custom_call" | custom-call | tf_op jit(solution)/shard_map/pallas_call | solution.py:299
  14.4 0.8 %shard_map.78 = (f32[1024,128]{1,0:T(8,128)}, f32[2,1,8]{2,1,0:T(1,128)}) custom-call(f32[1024,128]{1,0:T(8,128)S(1)} %get-tuple-element.6.history, f32[2,1,8]{2,1,0:T(1,128)S(1)} %get-tuple-element.7.record_range), custom_call_target="tpu_custom_call" | custom-call | tf_op jit(solution)/shard_map/pallas_call | solution.py:339

commit v5 on v4

--- a/solution.py
+++ b/solution.py
@@ -68,17 +68,6 @@
             skip = jnp.logical_and(b == lon_pos, jnp.logical_or(home, at_end))
             unless(skip, lambda b=b: signal(barrier, lon_pos * slab + x_pos, b))
 
-    for step in range(1, slab):
-        signal(barrier, plane * slab + lax.rem(x_pos + step, slab), lon_pos)
-    unless(jnp.logical_or(plane != last, collects), lambda: signal(barrier, lon_pos * slab + slab - 1, lon_pos))
-    unless(collects, lambda: signal(barrier, plane * slab + slab - 1, plane))
-    pl.when(collects)(lambda: signal(barrier, lat_pos, partner))
-
-    @pl.when(plane != last)
-    def _():
-        for step in range(1, planes):
-            signal(barrier, lax.rem(plane + step, planes) * slab + x_pos, lon_pos)
-
     smalls = [
         pltpu.make_async_copy(src, dst, in_sem.at[n])
         for n, (src, dst) in enumerate([
@@ -90,6 +79,17 @@
         copy.start()
     for n in range(levels):
         pltpu.make_async_copy(x_hbm.at[:, order(n)], xs.at[n], x_sem).start()
+    for step in range(1, slab):
+        signal(barrier, plane * slab + lax.rem(x_pos + step, slab), lon_pos)
+    unless(jnp.logical_or(plane != last, collects), lambda: signal(barrier, lon_pos * slab + slab - 1, lon_pos))
+    unless(collects, lambda: signal(barrier, plane * slab + slab - 1, plane))
+    pl.when(collects)(lambda: signal(barrier, lat_pos, partner))
+
+    @pl.when(plane != last)
+    def _():
+        for step in range(1, planes):
+            signal(barrier, lax.rem(plane + step, planes) * slab + x_pos, lon_pos)
+
     for copy in smalls:
         copy.wait()
 
@@ -152,8 +152,6 @@
     def unless_here(other, body):
         unless(other == plane, body)
 
-    loop(0, last, lambda other: unless_here(other, lambda: tell(other).start()))
-
     @pl.when(collects)
     def _():
         def pass_on(step):
@@ -166,6 +164,8 @@
     pl.when(helps)(lambda: signal(token, lat_pos, partner))
     for step in range(1, slab):
         signal(cross, plane * slab + lax.rem(x_pos + step, slab), lon_pos)
+
+    loop(0, last, lambda other: unless_here(other, lambda: tell(other).start()))
 
     def remote(n):
         return pltpu.make_async_remote_copy(
@@ -240,15 +240,33 @@
             line = line[:1, :fields]
             rng[end] = line if end == 0 else -line
 
-    per_field = (slab * rows) * lon_count
+    per_field = out.shape[0] // fields
     pairs = lon_count // 2
+    crossed = lower == (lon_pos >= planes // 2)
+
+    def drain():
+        pl.when(plane == last - 1)(forward.wait_send)
+
+        @pl.when(plane != last)
+        def _():
+            wait_rows(last_stats, sources - 1, last_send)
+            wait_rows(first_stats, last - 1, stat_send)
+
+        pl.when(plane == last)(lambda: wait_rows(first_stats, last, stat_send))
+        pl.when(home)(lambda: wait_rows(send, levels - 1, send_sem))
+        unless(home, lambda: wait_rows(send, levels, send_sem))
 
     for turn in range(sources):
-        core, j, i = 1 - turn // (pairs * slab), turn // slab % pairs, slab - 1 - turn % slab
+        core, i, j = 1 - turn // (pairs * slab), turn // pairs % slab, turn % pairs
         b = 2 * lax.rem(lon_pos // 2 + j, pairs) + core
         source = i * lon_count + b
+        if turn == 0:
+            pl.when(plane == last - 1)(finish_range)
+        if turn == sources // 2:
+            pl.when(jnp.logical_and(crossed, plane != last - 1))(finish_range)
         if turn == sources - 1:
-            finish_range()
+            pl.when(jnp.logical_not(jnp.logical_or(crossed, plane == last - 1)))(finish_range)
+            drain()
         unless(jnp.logical_and(home, source == here), lambda source=source: pltpu.make_async_copy(
             recv.at[source], recv.at[source], recv_sem.at[source]).wait())
         stage[source] = recv[source]
@@ -262,21 +280,10 @@
             out[pl.ds(start, fields, stride=per_field), :] = strip
             rank = rank + live
 
-    pl.when(plane == last - 1)(forward.wait_send)
-
-    @pl.when(plane != last)
-    def _():
-        wait_rows(last_stats, sources - 1, last_send)
-        wait_rows(first_stats, last - 1, stat_send)
-
-    pl.when(plane == last)(lambda: wait_rows(first_stats, last, stat_send))
-    pl.when(home)(lambda: wait_rows(send, levels - 1, send_sem))
-    unless(home, lambda: wait_rows(send, levels, send_sem))
-
 
 def store(history, record_range, history_out, record_range_out, sem):
     copies = [
-        pltpu.make_async_copy(history, history_out, sem.at[0]),
+        pltpu.make_async_copy(history.at[:, pl.ds(0, history_out.shape[1])], history_out, sem.at[0]),
         pltpu.make_async_copy(record_range, record_range_out, sem.at[1]),
     ]
     for copy in copies:
@@ -292,14 +299,14 @@
     slab = lat_count // lon_count
     slots = min(MAX_LIVE, rows)
     sources = slab * lon_count
-    out_rows = nfield * slab * rows * lon_count
+    per_field = slab * rows * lon_count
     stat_rows = 2 * levels * nfield // STRIP
     hbm = pl.BlockSpec(memory_space=pltpu.HBM)
     vmem = pl.BlockSpec(memory_space=pltpu.VMEM)
     history, record_range = pl.pallas_call(
         functools.partial(exchange, (nfield, levels, rows, lat_count, lon_count)),
         out_shape=(
-            pltpu.VMEM((out_rows, STRIP), jnp.float32),
+            pltpu.VMEM((nfield * (per_field + 8), STRIP), jnp.float32),
             pltpu.VMEM((2, 1, nfield), jnp.float32),
         ),
         in_specs=[hbm] * 6,
@@ -339,7 +346,7 @@
     history, record_range = pl.pallas_call(
         store,
         out_shape=(
-            jax.ShapeDtypeStruct(history.shape, jnp.float32),
+            jax.ShapeDtypeStruct((nfield, per_field, STRIP), jnp.float32),
             jax.ShapeDtypeStruct(record_range.shape, jnp.float32),
         ),
         in_specs=[vmem, vmem],
@@ -347,7 +354,7 @@
         scratch_shapes=[pltpu.SemaphoreType.DMA((2,))],
         compiler_params=pltpu.CompilerParams(vmem_limit_bytes=1 << 20),
     )(
-        pltpu.with_memory_space_constraint(history, pltpu.VMEM),
+        pltpu.with_memory_space_constraint(history.reshape(nfield, per_field + 8, STRIP), pltpu.VMEM),
         pltpu.with_memory_space_constraint(record_range, pltpu.VMEM),
     )
     history = history.reshape(nfield, slab * rows // 8, lon_count, 8, STRIP)

time: 15.4 us -> 15.1 us (0.981)
  the two profiles are of different devices: /device:TPU:4 before, /device:TPU:25 now
where the time goes in v5:
time: 15.1 us; the launch traced here: 14.8 us
  Pallas kernels  14.2 us (94%)
  between operations  0.64 us (4%)
    pallas_call x1, Pallas kernels, per_device(): pl.pallas_call(functools.partial(exchange, (nfield, levels, rows, lat_cou...  13.3 us
    pallas_call x1, Pallas kernels, per_device(): pl.pallas_call(store, out_shape=(jax.ShapeDtypeStruct((nfield, per_field,...  0.81 us

profile of v5, /device:TPU:25, one launch (start us, length us, event | category | flops | bytes accessed | tf_op | source)
XLA Modules:
  0.0 14.8 jit_solution(8003848109265693623)
XLA Ops:
  0.6 13.3 %shard_map.77 = (f32[1088,128]{1,0:T(8,128)S(1)}, f32[2,1,8]{2,1,0:T(1,128)S(1)}) custom-call(s32[4,128]{1,0:T(4,128)} %bitcast.11, f32[16]{0:T(128)} %scale_table_hbm.1, f32[16]{0:T(128)} %offset_table_hbm.1, s32[8]{0:T(128)} %scale_index_hbm.1, s32[8]{0:T(128)} %offset_index_hbm.1, f32[8,8,16,128]{3,2,1,0:T(8,128)} %x_hbm.1), custom_call_target="tpu_custom_call" | custom-call | tf_op jit(solution)/shard_map/pallas_call | solution.py:306
  14.0 0.8 %shard_map.78 = (f32[8,128,128]{2,1,0:T(8,128)}, f32[2,1,8]{2,1,0:T(1,128)}) custom-call(f32[8,136,128]{2,1,0:T(8,128)S(1)} %bitcast.10, f32[2,1,8]{2,1,0:T(1,128)S(1)} %get-tuple-element.7.record_range), custom_call_target="tpu_custom_call" | custom-call | tf_op jit(solution)/shard_map/pallas_call | solution.py:346

commit v6 on v5

--- a/solution.py
+++ b/solution.py
@@ -27,7 +27,7 @@
 def exchange(
     dims, mask_hbm, scale_table_hbm, offset_table_hbm, scale_index_hbm, offset_index_hbm, x_hbm,
     out, rng,
-    mask, scale_table, offset_table, scale_index, offset_index,
+    mask, scale_table, offset_table, scale_index, offset_index, after,
     xs, send, recv, stage, part, mine, first_stats, last_stats, best,
     x_sem, in_sem, send_sem, recv_sem, stat_send, stat_recv, last_send, last_recv, best_send, best_recv,
     token, cross,
@@ -77,8 +77,8 @@
     ]
     for copy in smalls:
         copy.start()
-    for n in range(levels):
-        pltpu.make_async_copy(x_hbm.at[:, order(n)], xs.at[n], x_sem).start()
+    for f in range(fields):
+        pltpu.make_async_copy(x_hbm.at[f], xs.at[:, :, f], x_sem).start()
     for step in range(1, slab):
         signal(barrier, plane * slab + lax.rem(x_pos + step, slab), lon_pos)
     unless(jnp.logical_or(plane != last, collects), lambda: signal(barrier, lon_pos * slab + slab - 1, lon_pos))
@@ -93,17 +93,17 @@
     for copy in smalls:
         copy.wait()
 
-    seen = []
-    total = jnp.int32(0)
-    for r in range(rows):
-        total = total + mask[lon_pos, lat_pos * rows + r]
-        seen.append(total)
-    picks = []
-    for k in range(slots):
-        pick = jnp.int32(k)
-        for r in range(k, rows - 1):
-            pick = pick + (seen[r] <= k).astype(jnp.int32)
-        picks.append(pick if k == 0 else jnp.where(k < total, pick, picks[-1]))
+    following = first = jnp.int32(0)
+    for r in reversed(range(rows)):
+        first = jnp.where(mask[lon_pos, lat_pos * rows + r] > 0, r, first)
+    following = first
+    after[rows] = first
+    for r in reversed(range(1, rows)):
+        following = jnp.where(mask[lon_pos, lat_pos * rows + r] > 0, r, following)
+        after[r] = following
+    picks = [first]
+    for k in range(1, slots):
+        picks.append(after[picks[-1] + 1])
 
     which = lax.broadcasted_iota(jnp.int32, (fields, STRIP), 0)
     scales = jnp.zeros((fields, STRIP), jnp.float32)
@@ -113,18 +113,16 @@
         offsets = jnp.where(which == f, offset_table[offset_index[f]], offsets)
 
     pltpu.make_async_copy(xs, xs, x_sem).wait()
-    lines = xs.reshape(levels * fields * rows, STRIP)
     for n in range(levels):
-        high = None
+        level = order(n)
+        high = low = None
         for k in range(slots):
-            strip = lines[pl.ds(n * fields * rows + picks[k], fields, stride=rows), :]
-            packed = (strip - offsets) * scales
+            packed = (xs[level, picks[k]] - offsets) * scales
             send[n, k] = packed
             high = packed if k == 0 else jnp.maximum(high, packed)
-            low = -packed if k == 0 else jnp.maximum(low, -packed)
-        level = order(n)
+            low = packed if k == 0 else jnp.minimum(low, packed)
         part[pl.ds(pl.multiple_of(level * fields, fields), fields), :] = high
-        part[pl.ds(pl.multiple_of((levels + level) * fields, fields), fields), :] = low
+        part[pl.ds(pl.multiple_of((levels + level) * fields, fields), fields), :] = -low
 
     for j in range(mine.shape[0]):
         tile = part[j * STRIP:(j + 1) * STRIP, :].T
@@ -317,7 +315,8 @@
             pltpu.SMEM(offset_table.shape, jnp.float32),
             pltpu.SMEM(scale_index.shape, jnp.int32),
             pltpu.SMEM(offset_index.shape, jnp.int32),
-            pltpu.VMEM((levels, nfield, rows, STRIP), jnp.float32),
+            pltpu.SMEM((rows + 1,), jnp.int32),
+            pltpu.VMEM((levels, rows, nfield, STRIP), jnp.float32),
             pltpu.VMEM((levels, slots, nfield, STRIP), jnp.float32),
             pltpu.VMEM((sources, slots, nfield, STRIP), jnp.float32),
             pltpu.VMEM((sources, slots, nfield, STRIP), jnp.float32),

time: 15.1 us -> 15 us (level)
  no operation moved by 1% of the time
where the time goes in v6:
time: 15 us; the launch traced here: 14.8 us
  Pallas kernels  14.2 us (95%)
  between operations  0.64 us (4%)
    pallas_call x1, Pallas kernels, per_device(): pl.pallas_call(functools.partial(exchange, (nfield, levels, rows, lat_cou...  13.3 us
    pallas_call x1, Pallas kernels, per_device(): pl.pallas_call(store, out_shape=(jax.ShapeDtypeStruct((nfield, per_field,...  0.81 us

profile of v6, /device:TPU:25, one launch (start us, length us, event | category | flops | bytes accessed | tf_op | source)
XLA Modules:
  0.0 14.8 jit_solution(12479527506881321741)
XLA Ops:
  0.6 13.3 %shard_map.77 = (f32[1088,128]{1,0:T(8,128)S(1)}, f32[2,1,8]{2,1,0:T(1,128)S(1)}) custom-call(s32[4,128]{1,0:T(4,128)} %bitcast.11, f32[16]{0:T(128)} %scale_table_hbm.1, f32[16]{0:T(128)} %offset_table_hbm.1, s32[8]{0:T(128)} %scale_index_hbm.1, s32[8]{0:T(128)} %offset_index_hbm.1, f32[8,8,16,128]{3,2,1,0:T(8,128)} %x_hbm.1), custom_call_target="tpu_custom_call" | custom-call | tf_op jit(solution)/shard_map/pallas_call | solution.py:304
  14.0 0.8 %shard_map.78 = (f32[8,128,128]{2,1,0:T(8,128)}, f32[2,1,8]{2,1,0:T(1,128)}) custom-call(f32[8,136,128]{2,1,0:T(8,128)S(1)} %bitcast.10, f32[2,1,8]{2,1,0:T(1,128)S(1)} %get-tuple-element.7.record_range), custom_call_target="tpu_custom_call" | custom-call | tf_op jit(solution)/shard_map/pallas_call | solution.py:345

commit v7 on v6

--- a/solution.py
+++ b/solution.py
@@ -29,7 +29,7 @@
     out, rng,
     mask, scale_table, offset_table, scale_index, offset_index, after,
     xs, send, recv, stage, part, mine, first_stats, last_stats, best,
-    x_sem, in_sem, send_sem, recv_sem, stat_send, stat_recv, last_send, last_recv, best_send, best_recv,
+    x_sem, in_sem, sent, recv_sem, stat_recv, last_recv, best_recv,
     token, cross,
 ):
     fields, levels, rows, lat_count, lon_count = dims
@@ -68,8 +68,13 @@
             skip = jnp.logical_and(b == lon_pos, jnp.logical_or(home, at_end))
             unless(skip, lambda b=b: signal(barrier, lon_pos * slab + x_pos, b))
 
+    @pl.when(plane != last)
+    def _():
+        for step in range(1, planes):
+            signal(barrier, lax.rem(plane + step, planes) * slab + x_pos, lon_pos)
+
     smalls = [
-        pltpu.make_async_copy(src, dst, in_sem.at[n])
+        pltpu.make_async_copy(src, dst, in_sem)
         for n, (src, dst) in enumerate([
             (mask_hbm, mask), (scale_table_hbm, scale_table), (offset_table_hbm, offset_table),
             (scale_index_hbm, scale_index), (offset_index_hbm, offset_index),
@@ -85,11 +90,6 @@
     unless(collects, lambda: signal(barrier, plane * slab + slab - 1, plane))
     pl.when(collects)(lambda: signal(barrier, lat_pos, partner))
 
-    @pl.when(plane != last)
-    def _():
-        for step in range(1, planes):
-            signal(barrier, lax.rem(plane + step, planes) * slab + x_pos, lon_pos)
-
     for copy in smalls:
         copy.wait()
 
@@ -144,7 +144,7 @@
 
     def tell(other):
         return row_copy(
-            mine, first_stats.at[plane], stat_send, stat_recv, other * slab + x_pos, lon_pos
+            mine, first_stats.at[plane], sent, stat_recv, other * slab + x_pos, lon_pos
         )
 
     def unless_here(other, body):
@@ -169,7 +169,7 @@
         return pltpu.make_async_remote_copy(
             src_ref=send.at[n],
             dst_ref=recv.at[here],
-            send_sem=send_sem,
+            send_sem=sent,
             recv_sem=recv_sem.at[here],
             device_id=(order(n), plane),
             device_id_type=MESH,
@@ -182,13 +182,15 @@
 
         loop(first, end, start)
 
+    below = jnp.where(lower, last - plane, last)
     post(0, 0, 1)
+    loop(below, last, lambda block: post(block, 0, 1))
     pl.semaphore_wait(cross, slab - 1)
     post(0, 1, slab)
 
     def post_block(block):
         post(block, 1, slab)
-        post(block, 0, 1)
+        unless(jnp.logical_and(block >= below, block < last), lambda: post(block, 0, 1))
 
     loop(1, last, post_block)
 
@@ -211,7 +213,7 @@
     def share(step):
         other = lax.rem(here + step, sources)
         return row_copy(
-            last_stats.at[here], last_stats.at[here], last_send, last_recv,
+            last_stats.at[here], last_stats.at[here], sent, last_recv,
             plane * slab + other // lon_count, lax.rem(other, lon_count),
         )
 
@@ -221,7 +223,7 @@
         last_stats[here] = jnp.max(first_stats[...], axis=0)
         loop(1, sources, lambda step: share(step).start())
 
-    forward = row_copy(best, best, best_send, best_recv, last * slab + x_pos, lon_pos)
+    forward = row_copy(best, best, sent, best_recv, last * slab + x_pos, lon_pos)
 
     def finish_range():
         @pl.when(plane != last)
@@ -247,12 +249,12 @@
 
         @pl.when(plane != last)
         def _():
-            wait_rows(last_stats, sources - 1, last_send)
-            wait_rows(first_stats, last - 1, stat_send)
-
-        pl.when(plane == last)(lambda: wait_rows(first_stats, last, stat_send))
-        pl.when(home)(lambda: wait_rows(send, levels - 1, send_sem))
-        unless(home, lambda: wait_rows(send, levels, send_sem))
+            wait_rows(last_stats, sources - 1, sent)
+            wait_rows(first_stats, last - 1, sent)
+
+        pl.when(plane == last)(lambda: wait_rows(first_stats, last, sent))
+        pl.when(home)(lambda: wait_rows(send, levels - 1, sent))
+        unless(home, lambda: wait_rows(send, levels, sent))
 
     for turn in range(sources):
         core, i, j = 1 - turn // (pairs * slab), turn // pairs % slab, turn % pairs
@@ -326,12 +328,9 @@
             pltpu.VMEM((sources, stat_rows, 1, STRIP), jnp.float32),
             pltpu.VMEM((stat_rows, 1, STRIP), jnp.float32),
             pltpu.SemaphoreType.DMA,
-            pltpu.SemaphoreType.DMA((5,)),
+            pltpu.SemaphoreType.DMA,
             pltpu.SemaphoreType.DMA,
             pltpu.SemaphoreType.DMA((sources,)),
-            pltpu.SemaphoreType.DMA,
-            pltpu.SemaphoreType.DMA,
-            pltpu.SemaphoreType.DMA,
             pltpu.SemaphoreType.DMA,
             pltpu.SemaphoreType.DMA,
             pltpu.SemaphoreType.DMA,

time: 15 us -> 14.9 us (level)
  no operation moved by 1% of the time
where the time goes in v7:
time: 14.9 us; the launch traced here: 14.8 us
  Pallas kernels  14.1 us (95%)
  between operations  0.64 us (4%)
    pallas_call x1, Pallas kernels, per_device(): pl.pallas_call(functools.partial(exchange, (nfield, levels, rows, lat_cou...  13.3 us
    pallas_call x1, Pallas kernels, per_device(): pl.pallas_call(store, out_shape=(jax.ShapeDtypeStruct((nfield, per_field,...  0.81 us

profile of v7, /device:TPU:25, one launch (start us, length us, event | category | flops | bytes accessed | tf_op | source)
XLA Modules:
  0.0 14.8 jit_solution(8811171477204195209)
XLA Ops:
  0.6 13.3 %shard_map.77 = (f32[1088,128]{1,0:T(8,128)S(1)}, f32[2,1,8]{2,1,0:T(1,128)S(1)}) custom-call(s32[4,128]{1,0:T(4,128)} %bitcast.11, f32[16]{0:T(128)} %scale_table_hbm.1, f32[16]{0:T(128)} %offset_table_hbm.1, s32[8]{0:T(128)} %scale_index_hbm.1, s32[8]{0:T(128)} %offset_index_hbm.1, f32[8,8,16,128]{3,2,1,0:T(8,128)} %x_hbm.1), custom_call_target="tpu_custom_call" | custom-call | tf_op jit(solution)/shard_map/pallas_call | solution.py:306
  13.9 0.8 %shard_map.78 = (f32[8,128,128]{2,1,0:T(8,128)}, f32[2,1,8]{2,1,0:T(1,128)}) custom-call(f32[8,136,128]{2,1,0:T(8,128)S(1)} %bitcast.10, f32[2,1,8]{2,1,0:T(1,128)S(1)} %get-tuple-element.7.record_range), custom_call_target="tpu_custom_call" | custom-call | tf_op jit(solution)/shard_map/pallas_call | solution.py:344

commit v8 on v7

--- a/solution.py
+++ b/solution.py
@@ -183,10 +183,12 @@
         loop(first, end, start)
 
     below = jnp.where(lower, last - plane, last)
-    post(0, 0, 1)
+    aside = jnp.logical_and(plane == planes // 2, jnp.logical_and(lax.rem(lon_pos, 2) == 0, at_end))
+    unless(aside, lambda: post(0, 0, 1))
     loop(below, last, lambda block: post(block, 0, 1))
     pl.semaphore_wait(cross, slab - 1)
     post(0, 1, slab)
+    pl.when(aside)(lambda: post(0, 0, 1))
 
     def post_block(block):
         post(block, 1, slab)

time: 14.9 us -> 14.9 us (level)
  no operation moved by 1% of the time
where the time goes in v8:
time: 14.9 us; the launch traced here: 14.8 us
  Pallas kernels  14.1 us (95%)
  between operations  0.64 us (4%)
    pallas_call x1, Pallas kernels, per_device(): pl.pallas_call(functools.partial(exchange, (nfield, levels, rows, lat_cou...  13.3 us
    pallas_call x1, Pallas kernels, per_device(): pl.pallas_call(store, out_shape=(jax.ShapeDtypeStruct((nfield, per_field,...  0.81 us

profile of v8, /device:TPU:25, one launch (start us, length us, event | category | flops | bytes accessed | tf_op | source)
XLA Modules:
  0.0 14.8 jit_solution(12348075328050580348)
XLA Ops:
  0.6 13.3 %shard_map.77 = (f32[1088,128]{1,0:T(8,128)S(1)}, f32[2,1,8]{2,1,0:T(1,128)S(1)}) custom-call(s32[4,128]{1,0:T(4,128)} %bitcast.11, f32[16]{0:T(128)} %scale_table_hbm.1, f32[16]{0:T(128)} %offset_table_hbm.1, s32[8]{0:T(128)} %scale_index_hbm.1, s32[8]{0:T(128)} %offset_index_hbm.1, f32[8,8,16,128]{3,2,1,0:T(8,128)} %x_hbm.1), custom_call_target="tpu_custom_call" | custom-call | tf_op jit(solution)/shard_map/pallas_call | solution.py:308
  13.9 0.8 %shard_map.78 = (f32[8,128,128]{2,1,0:T(8,128)}, f32[2,1,8]{2,1,0:T(1,128)}) custom-call(f32[8,136,128]{2,1,0:T(8,128)S(1)} %bitcast.10, f32[2,1,8]{2,1,0:T(1,128)S(1)} %get-tuple-element.7.record_range), custom_call_target="tpu_custom_call" | custom-call | tf_op jit(solution)/shard_map/pallas_call | solution.py:346

commit v9 on v8

--- a/solution.py
+++ b/solution.py
@@ -242,7 +242,6 @@
             line = line[:1, :fields]
             rng[end] = line if end == 0 else -line
 
-    per_field = out.shape[0] // fields
     pairs = lon_count // 2
     crossed = lower == (lon_pos >= planes // 2)
 
@@ -259,7 +258,7 @@
         unless(home, lambda: wait_rows(send, levels, sent))
 
     for turn in range(sources):
-        core, i, j = 1 - turn // (pairs * slab), turn // pairs % slab, turn % pairs
+        core, j, i = 1 - turn // (pairs * slab), turn // slab % pairs, turn % slab
         b = 2 * lax.rem(lon_pos // 2 + j, pairs) + core
         source = i * lon_count + b
         if turn == 0:
@@ -279,19 +278,20 @@
             strip = jnp.where(live > 0, strip, 0.0)
             line = i * rows + r
             start = (line // 8 * lon_count + b) * 8 + line % 8
-            out[pl.ds(start, fields, stride=per_field), :] = strip
+            out[start] = strip
             rank = rank + live
 
 
 def store(history, record_range, history_out, record_range_out, sem):
     copies = [
-        pltpu.make_async_copy(history.at[:, pl.ds(0, history_out.shape[1])], history_out, sem.at[0]),
-        pltpu.make_async_copy(record_range, record_range_out, sem.at[1]),
+        pltpu.make_async_copy(history.at[:, f], history_out.at[f], sem.at[0])
+        for f in range(history_out.shape[0])
     ]
+    copies.append(pltpu.make_async_copy(record_range, record_range_out, sem.at[1]))
     for copy in copies:
         copy.start()
-    for copy in copies:
-        copy.wait()
+    pltpu.make_async_copy(history, history, sem.at[0]).wait()
+    copies[-1].wait()
 
 
 def per_device(fields, ocean_mask, scale_table, offset_table, scale_index, offset_index):
@@ -308,7 +308,7 @@
     history, record_range = pl.pallas_call(
         functools.partial(exchange, (nfield, levels, rows, lat_count, lon_count)),
         out_shape=(
-            pltpu.VMEM((nfield * (per_field + 8), STRIP), jnp.float32),
+            pltpu.VMEM((per_field, nfield, STRIP), jnp.float32),
             pltpu.VMEM((2, 1, nfield), jnp.float32),
         ),
         in_specs=[hbm] * 6,
@@ -354,7 +354,7 @@
         scratch_shapes=[pltpu.SemaphoreType.DMA((2,))],
         compiler_params=pltpu.CompilerParams(vmem_limit_bytes=1 << 20),
     )(
-        pltpu.with_memory_space_constraint(history.reshape(nfield, per_field + 8, STRIP), pltpu.VMEM),
+        pltpu.with_memory_space_constraint(history, pltpu.VMEM),
         pltpu.with_memory_space_constraint(record_range, pltpu.VMEM),
     )
     history = history.reshape(nfield, slab * rows // 8, lon_count, 8, STRIP)

time: 14.9 us -> 14.9 us (level)
  no operation moved by 1% of the time
where the time goes in v9:
time: 14.9 us; the launch traced here: 14.7 us
  Pallas kernels  14 us (94%)
  between operations  0.64 us (4%)
    pallas_call x1, Pallas kernels, per_device(): pl.pallas_call(functools.partial(exchange, (nfield, levels, rows, lat_cou...  13.2 us
    pallas_call x1, Pallas kernels, per_device(): pl.pallas_call(store, out_shape=(jax.ShapeDtypeStruct((nfield, per_field,...  0.8 us

profile of v9, /device:TPU:25, one launch (start us, length us, event | category | flops | bytes accessed | tf_op | source)
XLA Modules:
  0.0 14.7 jit_solution(11424881372541764472)
XLA Ops:
  0.6 13.2 %shard_map.77 = (f32[128,8,128]{2,1,0:T(8,128)S(1)}, f32[2,1,8]{2,1,0:T(1,128)S(1)}) custom-call(s32[4,128]{1,0:T(4,128)} %bitcast.9, f32[16]{0:T(128)} %scale_table_hbm.1, f32[16]{0:T(128)} %offset_table_hbm.1, s32[8]{0:T(128)} %scale_index_hbm.1, s32[8]{0:T(128)} %offset_index_hbm.1, f32[8,8,16,128]{3,2,1,0:T(8,128)} %x_hbm.1), custom_call_target="tpu_custom_call" | custom-call | tf_op jit(solution)/shard_map/pallas_call | solution.py:308
  13.9 0.8 %shard_map.78 = (f32[8,128,128]{2,1,0:T(8,128)}, f32[2,1,8]{2,1,0:T(1,128)}) custom-call(f32[128,8,128]{2,1,0:T(8,128)S(1)} %get-tuple-element.6.history, f32[2,1,8]{2,1,0:T(1,128)S(1)} %get-tuple-element.7.record_range), custom_call_target="tpu_custom_call" | custom-call | tf_op jit(solution)/shard_map/pallas_call | solution.py:346
